TPU v7x, 64 devices: a 2x2x8 block of a 4x4x8 slice. The times are simulated.
64 devices in a mesh: rep: 4 (over x, y), shard: 16 (over z, core).
Axes of the slice: x: 2, y: 2, z: 8, core: 2. Of those that a mesh axis runs over, the one named last changes fastest.
The devices are a block of a 4x4x8 slice.
Arguments:
- ratings: float32 [4096, 8192], P(('rep', 'shard')), parts along dimension 0
- observed: int32 [4096, 8192], P(('rep', 'shard')), parts along dimension 0
- user_init: float32 [4096, 128], P(('rep', 'shard')), parts along dimension 0
- item_init: float32 [32768, 128], P(('rep', 'shard')), parts along dimension 0
Outputs:
- output 1: float32 [4096, 128], P(('rep', 'shard')), parts along dimension 0
- output 2: float32 [32768, 128], P(('rep', 'shard')), parts along dimension 0
There are 4 independent parts. A program takes and returns all parts, laid end to end along the dimension named above; each array names one.
All inputs are finite; a program needn't handle non-finite values.
Results may differ from a plain program's by a relative error of at most 0.00268177.
Values are sent between devices in bfloat16 or wider.
A program may use at most 768 MiB of HBM per device.

v0:
```python
import jax
import jax.numpy as jnp
import math
from jax import lax
from jax.sharding import PartitionSpec as P

STRATUM_STEPS = 4
EPOCHS = 2


def solution(mesh):
    group_devs = mesh.shape["shard"]
    row_spec = P(("rep", "shard"), None)
    shift_back = [(source, (source - 1) % group_devs) for source in range(group_devs)]

    def local(ratings, observed, user_init, item_init):
        users_dev = ratings.shape[0]
        items_dev, factor_rank = item_init.shape
        step_scale = (users_dev + items_dev + factor_rank) / math.sqrt(factor_rank)
        step_size = 0.5 / step_scale
        weight_decay = 0.03 * math.sqrt(users_dev * items_dev / factor_rank)
        seen_all = observed != 0
        my_index = lax.axis_index("shard")

        def stratum(stratum_idx, state_pair):
            user_blk, item_blk = state_pair
            col_start = ((my_index + stratum_idx) % group_devs) * items_dev
            rating_blk = lax.dynamic_slice_in_dim(ratings, col_start, items_dev, axis=1)
            seen_blk = lax.dynamic_slice_in_dim(seen_all, col_start, items_dev, axis=1)

            def step(unused, inner_pair):
                user_cur, item_cur = inner_pair
                item_bf = item_cur.astype(jnp.bfloat16)
                predicted = jnp.einsum("ur,ir->ui", user_cur.astype(jnp.bfloat16), item_bf, preferred_element_type=jnp.float32)
                residual = jnp.where(seen_blk, predicted - rating_blk, 0.0).astype(jnp.bfloat16)
                grad_user = jnp.dot(residual, item_bf, preferred_element_type=jnp.float32)
                user_new = user_cur - step_size * (grad_user + weight_decay * user_cur)
                user_bf = user_new.astype(jnp.bfloat16)
                predicted = jnp.einsum("ur,ir->ui", user_bf, item_bf, preferred_element_type=jnp.float32)
                residual = jnp.where(seen_blk, predicted - rating_blk, 0.0).astype(jnp.bfloat16)
                grad_item = jnp.einsum("ui,ur->ir", residual, user_bf, preferred_element_type=jnp.float32)
                item_new = item_cur - step_size * (grad_item + weight_decay * item_cur)
                return user_new, item_new

            user_blk, item_blk = lax.fori_loop(0, STRATUM_STEPS, step, (user_blk, item_blk))
            item_blk = lax.ppermute(item_blk, "shard", shift_back)
            return user_blk, item_blk

        return lax.fori_loop(0, EPOCHS * group_devs, stratum, (user_init, item_init))

    return jax.shard_map(local, mesh=mesh, in_specs=(row_spec, row_spec, row_spec, row_spec), out_specs=(row_spec, row_spec), check_vma=False)
```

profile of v0, /device:TPU:21, one launch (start us, length us, event | category | flops | bytes accessed | tf_op | source)
XLA Modules:
  0.0 357.2 jit_solution(6671926228158959292)
XLA Ops:
  2.6 353.9 %while.53 = (s32[]{:T(128)}, f32[64,128]{1,0:T(8,128)S(1)}, f32[512,128]{1,0:T(8,128)S(1)}, s32[]{:T(128)}, f32[64,8192]{1,0:T(8,128)}, /*index=5*/pred[64,8192]...) while((s32[]{:T(128)}, f32[64,128]{1,0:T(8,128)S(1)}, ...), condition=%wide.region_3.4_spmd, body=%wide.region_0.3_spmd.sunk | while | flops 34267152 | bytes 3703249 | solution.py:49
  17.9 4.9 %collective-permute-start = (f32[512,128]{1,0:T(8,128)S(1)}, f32[512,128]{1,0:T(8,128)S(1)}, u32[]{:S(2)}, u32[]{:S(2)}) collective-permute-start(f32[512,128]{1,0:T(8,128)S(1)} %get-tuple-element.291), channel_id=1, source_target_pairs={{0,15},{1,0},{2,1},{3,2},{4,3},{5,4},{6,5},{7,6},{8,7},{9,8},{10,9... | collective-permute-start | bytes 786440 | tf_op jit(solution)/shard_map/while/body/eval_jaxpr/ppermute | solution.py:46
  28.0 5.9 %collective-permute-start = (f32[512,128]{1,0:T(8,128)S(1)}, f32[512,128]{1,0:T(8,128)S(1)}, u32[]{:S(2)}, u32[]{:S(2)}) collective-permute-start(f32[512,128]{1,0:T(8,128)S(1)} %get-tuple-element.291), channel_id=1, source_target_pairs={{0,15},{1,0},{2,1},{3,2},{4,3},{5,4},{6,5},{7,6},{8,7},{9,8},{10,9... | collective-permute-start | bytes 786440 | tf_op jit(solution)/shard_map/while/body/eval_jaxpr/ppermute | solution.py:46
  39.1 5.9 %collective-permute-start = (f32[512,128]{1,0:T(8,128)S(1)}, f32[512,128]{1,0:T(8,128)S(1)}, u32[]{:S(2)}, u32[]{:S(2)}) collective-permute-start(f32[512,128]{1,0:T(8,128)S(1)} %get-tuple-element.291), channel_id=1, source_target_pairs={{0,15},{1,0},{2,1},{3,2},{4,3},{5,4},{6,5},{7,6},{8,7},{9,8},{10,9... | collective-permute-start | bytes 786440 | tf_op jit(solution)/shard_map/while/body/eval_jaxpr/ppermute | solution.py:46
  50.1 5.9 %collective-permute-start = (f32[512,128]{1,0:T(8,128)S(1)}, f32[512,128]{1,0:T(8,128)S(1)}, u32[]{:S(2)}, u32[]{:S(2)}) collective-permute-start(f32[512,128]{1,0:T(8,128)S(1)} %get-tuple-element.291), channel_id=1, source_target_pairs={{0,15},{1,0},{2,1},{3,2},{4,3},{5,4},{6,5},{7,6},{8,7},{9,8},{10,9... | collective-permute-start | bytes 786440 | tf_op jit(solution)/shard_map/while/body/eval_jaxpr/ppermute | solution.py:46
  61.2 5.9 %collective-permute-start = (f32[512,128]{1,0:T(8,128)S(1)}, f32[512,128]{1,0:T(8,128)S(1)}, u32[]{:S(2)}, u32[]{:S(2)}) collective-permute-start(f32[512,128]{1,0:T(8,128)S(1)} %get-tuple-element.291), channel_id=1, source_target_pairs={{0,15},{1,0},{2,1},{3,2},{4,3},{5,4},{6,5},{7,6},{8,7},{9,8},{10,9... | collective-permute-start | bytes 786440 | tf_op jit(solution)/shard_map/while/body/eval_jaxpr/ppermute | solution.py:46
  72.3 5.9 %collective-permute-start = (f32[512,128]{1,0:T(8,128)S(1)}, f32[512,128]{1,0:T(8,128)S(1)}, u32[]{:S(2)}, u32[]{:S(2)}) collective-permute-start(f32[512,128]{1,0:T(8,128)S(1)} %get-tuple-element.291), channel_id=1, source_target_pairs={{0,15},{1,0},{2,1},{3,2},{4,3},{5,4},{6,5},{7,6},{8,7},{9,8},{10,9... | collective-permute-start | bytes 786440 | tf_op jit(solution)/shard_map/while/body/eval_jaxpr/ppermute | solution.py:46
  83.4 5.9 %collective-permute-start = (f32[512,128]{1,0:T(8,128)S(1)}, f32[512,128]{1,0:T(8,128)S(1)}, u32[]{:S(2)}, u32[]{:S(2)}) collective-permute-start(f32[512,128]{1,0:T(8,128)S(1)} %get-tuple-element.291), channel_id=1, source_target_pairs={{0,15},{1,0},{2,1},{3,2},{4,3},{5,4},{6,5},{7,6},{8,7},{9,8},{10,9... | collective-permute-start | bytes 786440 | tf_op jit(solution)/shard_map/while/body/eval_jaxpr/ppermute | solution.py:46
  94.5 5.9 %collective-permute-start = (f32[512,128]{1,0:T(8,128)S(1)}, f32[512,128]{1,0:T(8,128)S(1)}, u32[]{:S(2)}, u32[]{:S(2)}) collective-permute-start(f32[512,128]{1,0:T(8,128)S(1)} %get-tuple-element.291), channel_id=1, source_target_pairs={{0,15},{1,0},{2,1},{3,2},{4,3},{5,4},{6,5},{7,6},{8,7},{9,8},{10,9... | collective-permute-start | bytes 786440 | tf_op jit(solution)/shard_map/while/body/eval_jaxpr/ppermute | solution.py:46
  105.6 5.9 %collective-permute-start = (f32[512,128]{1,0:T(8,128)S(1)}, f32[512,128]{1,0:T(8,128)S(1)}, u32[]{:S(2)}, u32[]{:S(2)}) collective-permute-start(f32[512,128]{1,0:T(8,128)S(1)} %get-tuple-element.291), channel_id=1, source_target_pairs={{0,15},{1,0},{2,1},{3,2},{4,3},{5,4},{6,5},{7,6},{8,7},{9,8},{10,9... | collective-permute-start | bytes 786440 | tf_op jit(solution)/shard_map/while/body/eval_jaxpr/ppermute | solution.py:46
  116.6 5.9 %collective-permute-start = (f32[512,128]{1,0:T(8,128)S(1)}, f32[512,128]{1,0:T(8,128)S(1)}, u32[]{:S(2)}, u32[]{:S(2)}) collective-permute-start(f32[512,128]{1,0:T(8,128)S(1)} %get-tuple-element.291), channel_id=1, source_target_pairs={{0,15},{1,0},{2,1},{3,2},{4,3},{5,4},{6,5},{7,6},{8,7},{9,8},{10,9... | collective-permute-start | bytes 786440 | tf_op jit(solution)/shard_map/while/body/eval_jaxpr/ppermute | solution.py:46
  127.7 5.9 %collective-permute-start = (f32[512,128]{1,0:T(8,128)S(1)}, f32[512,128]{1,0:T(8,128)S(1)}, u32[]{:S(2)}, u32[]{:S(2)}) collective-permute-start(f32[512,128]{1,0:T(8,128)S(1)} %get-tuple-element.291), channel_id=1, source_target_pairs={{0,15},{1,0},{2,1},{3,2},{4,3},{5,4},{6,5},{7,6},{8,7},{9,8},{10,9... | collective-permute-start | bytes 786440 | tf_op jit(solution)/shard_map/while/body/eval_jaxpr/ppermute | solution.py:46
  138.8 5.9 %collective-permute-start = (f32[512,128]{1,0:T(8,128)S(1)}, f32[512,128]{1,0:T(8,128)S(1)}, u32[]{:S(2)}, u32[]{:S(2)}) collective-permute-start(f32[512,128]{1,0:T(8,128)S(1)} %get-tuple-element.291), channel_id=1, source_target_pairs={{0,15},{1,0},{2,1},{3,2},{4,3},{5,4},{6,5},{7,6},{8,7},{9,8},{10,9... | collective-permute-start | bytes 786440 | tf_op jit(solution)/shard_map/while/body/eval_jaxpr/ppermute | solution.py:46
  149.9 5.9 %collective-permute-start = (f32[512,128]{1,0:T(8,128)S(1)}, f32[512,128]{1,0:T(8,128)S(1)}, u32[]{:S(2)}, u32[]{:S(2)}) collective-permute-start(f32[512,128]{1,0:T(8,128)S(1)} %get-tuple-element.291), channel_id=1, source_target_pairs={{0,15},{1,0},{2,1},{3,2},{4,3},{5,4},{6,5},{7,6},{8,7},{9,8},{10,9... | collective-permute-start | bytes 786440 | tf_op jit(solution)/shard_map/while/body/eval_jaxpr/ppermute | solution.py:46
  161.0 5.9 %collective-permute-start = (f32[512,128]{1,0:T(8,128)S(1)}, f32[512,128]{1,0:T(8,128)S(1)}, u32[]{:S(2)}, u32[]{:S(2)}) collective-permute-start(f32[512,128]{1,0:T(8,128)S(1)} %get-tuple-element.291), channel_id=1, source_target_pairs={{0,15},{1,0},{2,1},{3,2},{4,3},{5,4},{6,5},{7,6},{8,7},{9,8},{10,9... | collective-permute-start | bytes 786440 | tf_op jit(solution)/shard_map/while/body/eval_jaxpr/ppermute | solution.py:46
  172.1 5.9 %collective-permute-start = (f32[512,128]{1,0:T(8,128)S(1)}, f32[512,128]{1,0:T(8,128)S(1)}, u32[]{:S(2)}, u32[]{:S(2)}) collective-permute-start(f32[512,128]{1,0:T(8,128)S(1)} %get-tuple-element.291), channel_id=1, source_target_pairs={{0,15},{1,0},{2,1},{3,2},{4,3},{5,4},{6,5},{7,6},{8,7},{9,8},{10,9... | collective-permute-start | bytes 786440 | tf_op jit(solution)/shard_map/while/body/eval_jaxpr/ppermute | solution.py:46
  183.1 5.9 %collective-permute-start = (f32[512,128]{1,0:T(8,128)S(1)}, f32[512,128]{1,0:T(8,128)S(1)}, u32[]{:S(2)}, u32[]{:S(2)}) collective-permute-start(f32[512,128]{1,0:T(8,128)S(1)} %get-tuple-element.291), channel_id=1, source_target_pairs={{0,15},{1,0},{2,1},{3,2},{4,3},{5,4},{6,5},{7,6},{8,7},{9,8},{10,9... | collective-permute-start | bytes 786440 | tf_op jit(solution)/shard_map/while/body/eval_jaxpr/ppermute | solution.py:46
  194.2 5.9 %collective-permute-start = (f32[512,128]{1,0:T(8,128)S(1)}, f32[512,128]{1,0:T(8,128)S(1)}, u32[]{:S(2)}, u32[]{:S(2)}) collective-permute-start(f32[512,128]{1,0:T(8,128)S(1)} %get-tuple-element.291), channel_id=1, source_target_pairs={{0,15},{1,0},{2,1},{3,2},{4,3},{5,4},{6,5},{7,6},{8,7},{9,8},{10,9... | collective-permute-start | bytes 786440 | tf_op jit(solution)/shard_map/while/body/eval_jaxpr/ppermute | solution.py:46
  205.3 5.9 %collective-permute-start = (f32[512,128]{1,0:T(8,128)S(1)}, f32[512,128]{1,0:T(8,128)S(1)}, u32[]{:S(2)}, u32[]{:S(2)}) collective-permute-start(f32[512,128]{1,0:T(8,128)S(1)} %get-tuple-element.291), channel_id=1, source_target_pairs={{0,15},{1,0},{2,1},{3,2},{4,3},{5,4},{6,5},{7,6},{8,7},{9,8},{10,9... | collective-permute-start | bytes 786440 | tf_op jit(solution)/shard_map/while/body/eval_jaxpr/ppermute | solution.py:46
  216.4 5.9 %collective-permute-start = (f32[512,128]{1,0:T(8,128)S(1)}, f32[512,128]{1,0:T(8,128)S(1)}, u32[]{:S(2)}, u32[]{:S(2)}) collective-permute-start(f32[512,128]{1,0:T(8,128)S(1)} %get-tuple-element.291), channel_id=1, source_target_pairs={{0,15},{1,0},{2,1},{3,2},{4,3},{5,4},{6,5},{7,6},{8,7},{9,8},{10,9... | collective-permute-start | bytes 786440 | tf_op jit(solution)/shard_map/while/body/eval_jaxpr/ppermute | solution.py:46
  227.5 5.9 %collective-permute-start = (f32[512,128]{1,0:T(8,128)S(1)}, f32[512,128]{1,0:T(8,128)S(1)}, u32[]{:S(2)}, u32[]{:S(2)}) collective-permute-start(f32[512,128]{1,0:T(8,128)S(1)} %get-tuple-element.291), channel_id=1, source_target_pairs={{0,15},{1,0},{2,1},{3,2},{4,3},{5,4},{6,5},{7,6},{8,7},{9,8},{10,9... | collective-permute-start | bytes 786440 | tf_op jit(solution)/shard_map/while/body/eval_jaxpr/ppermute | solution.py:46
  238.5 5.9 %collective-permute-start = (f32[512,128]{1,0:T(8,128)S(1)}, f32[512,128]{1,0:T(8,128)S(1)}, u32[]{:S(2)}, u32[]{:S(2)}) collective-permute-start(f32[512,128]{1,0:T(8,128)S(1)} %get-tuple-element.291), channel_id=1, source_target_pairs={{0,15},{1,0},{2,1},{3,2},{4,3},{5,4},{6,5},{7,6},{8,7},{9,8},{10,9... | collective-permute-start | bytes 786440 | tf_op jit(solution)/shard_map/while/body/eval_jaxpr/ppermute | solution.py:46
  249.6 5.9 %collective-permute-start = (f32[512,128]{1,0:T(8,128)S(1)}, f32[512,128]{1,0:T(8,128)S(1)}, u32[]{:S(2)}, u32[]{:S(2)}) collective-permute-start(f32[512,128]{1,0:T(8,128)S(1)} %get-tuple-element.291), channel_id=1, source_target_pairs={{0,15},{1,0},{2,1},{3,2},{4,3},{5,4},{6,5},{7,6},{8,7},{9,8},{10,9... | collective-permute-start | bytes 786440 | tf_op jit(solution)/shard_map/while/body/eval_jaxpr/ppermute | solution.py:46
  260.7 5.9 %collective-permute-start = (f32[512,128]{1,0:T(8,128)S(1)}, f32[512,128]{1,0:T(8,128)S(1)}, u32[]{:S(2)}, u32[]{:S(2)}) collective-permute-start(f32[512,128]{1,0:T(8,128)S(1)} %get-tuple-element.291), channel_id=1, source_target_pairs={{0,15},{1,0},{2,1},{3,2},{4,3},{5,4},{6,5},{7,6},{8,7},{9,8},{10,9... | collective-permute-start | bytes 786440 | tf_op jit(solution)/shard_map/while/body/eval_jaxpr/ppermute | solution.py:46
  271.8 5.9 %collective-permute-start = (f32[512,128]{1,0:T(8,128)S(1)}, f32[512,128]{1,0:T(8,128)S(1)}, u32[]{:S(2)}, u32[]{:S(2)}) collective-permute-start(f32[512,128]{1,0:T(8,128)S(1)} %get-tuple-element.291), channel_id=1, source_target_pairs={{0,15},{1,0},{2,1},{3,2},{4,3},{5,4},{6,5},{7,6},{8,7},{9,8},{10,9... | collective-permute-start | bytes 786440 | tf_op jit(solution)/shard_map/while/body/eval_jaxpr/ppermute | solution.py:46
  282.9 5.9 %collective-permute-start = (f32[512,128]{1,0:T(8,128)S(1)}, f32[512,128]{1,0:T(8,128)S(1)}, u32[]{:S(2)}, u32[]{:S(2)}) collective-permute-start(f32[512,128]{1,0:T(8,128)S(1)} %get-tuple-element.291), channel_id=1, source_target_pairs={{0,15},{1,0},{2,1},{3,2},{4,3},{5,4},{6,5},{7,6},{8,7},{9,8},{10,9... | collective-permute-start | bytes 786440 | tf_op jit(solution)/shard_map/while/body/eval_jaxpr/ppermute | solution.py:46
  294.0 5.9 %collective-permute-start = (f32[512,128]{1,0:T(8,128)S(1)}, f32[512,128]{1,0:T(8,128)S(1)}, u32[]{:S(2)}, u32[]{:S(2)}) collective-permute-start(f32[512,128]{1,0:T(8,128)S(1)} %get-tuple-element.291), channel_id=1, source_target_pairs={{0,15},{1,0},{2,1},{3,2},{4,3},{5,4},{6,5},{7,6},{8,7},{9,8},{10,9... | collective-permute-start | bytes 786440 | tf_op jit(solution)/shard_map/while/body/eval_jaxpr/ppermute | solution.py:46
  305.0 5.9 %collective-permute-start = (f32[512,128]{1,0:T(8,128)S(1)}, f32[512,128]{1,0:T(8,128)S(1)}, u32[]{:S(2)}, u32[]{:S(2)}) collective-permute-start(f32[512,128]{1,0:T(8,128)S(1)} %get-tuple-element.291), channel_id=1, source_target_pairs={{0,15},{1,0},{2,1},{3,2},{4,3},{5,4},{6,5},{7,6},{8,7},{9,8},{10,9... | collective-permute-start | bytes 786440 | tf_op jit(solution)/shard_map/while/body/eval_jaxpr/ppermute | solution.py:46
  316.1 5.9 %collective-permute-start = (f32[512,128]{1,0:T(8,128)S(1)}, f32[512,128]{1,0:T(8,128)S(1)}, u32[]{:S(2)}, u32[]{:S(2)}) collective-permute-start(f32[512,128]{1,0:T(8,128)S(1)} %get-tuple-element.291), channel_id=1, source_target_pairs={{0,15},{1,0},{2,1},{3,2},{4,3},{5,4},{6,5},{7,6},{8,7},{9,8},{10,9... | collective-permute-start | bytes 786440 | tf_op jit(solution)/shard_map/while/body/eval_jaxpr/ppermute | solution.py:46
  327.2 5.9 %collective-permute-start = (f32[512,128]{1,0:T(8,128)S(1)}, f32[512,128]{1,0:T(8,128)S(1)}, u32[]{:S(2)}, u32[]{:S(2)}) collective-permute-start(f32[512,128]{1,0:T(8,128)S(1)} %get-tuple-element.291), channel_id=1, source_target_pairs={{0,15},{1,0},{2,1},{3,2},{4,3},{5,4},{6,5},{7,6},{8,7},{9,8},{10,9... | collective-permute-start | bytes 786440 | tf_op jit(solution)/shard_map/while/body/eval_jaxpr/ppermute | solution.py:46
  338.3 5.9 %collective-permute-start = (f32[512,128]{1,0:T(8,128)S(1)}, f32[512,128]{1,0:T(8,128)S(1)}, u32[]{:S(2)}, u32[]{:S(2)}) collective-permute-start(f32[512,128]{1,0:T(8,128)S(1)} %get-tuple-element.291), channel_id=1, source_target_pairs={{0,15},{1,0},{2,1},{3,2},{4,3},{5,4},{6,5},{7,6},{8,7},{9,8},{10,9... | collective-permute-start | bytes 786440 | tf_op jit(solution)/shard_map/while/body/eval_jaxpr/ppermute | solution.py:46
  349.4 5.9 %collective-permute-start = (f32[512,128]{1,0:T(8,128)S(1)}, f32[512,128]{1,0:T(8,128)S(1)}, u32[]{:S(2)}, u32[]{:S(2)}) collective-permute-start(f32[512,128]{1,0:T(8,128)S(1)} %get-tuple-element.291), channel_id=1, source_target_pairs={{0,15},{1,0},{2,1},{3,2},{4,3},{5,4},{6,5},{7,6},{8,7},{9,8},{10,9... | collective-permute-start | bytes 786440 | tf_op jit(solution)/shard_map/while/body/eval_jaxpr/ppermute | solution.py:46
  (682 shorter events, 263.5 us)
Async XLA Ops:
  6.6 7.3 %collective-permute-start = (f32[512,128]{1,0:T(8,128)S(1)}, f32[512,128]{1,0:T(8,128)S(1)}, u32[]{:S(2)}, u32[]{:S(2)}) collective-permute-start(f32[512,128]{1,0:T(8,128)S(1)} %get-tuple-element.291), channel_id=1, source_target_pairs={{0,15},{1,0},{2,1},{3,2},{4,3},{5,4},{6,5},{7,6},{8,7},{9,8},{10,9... | collective-permute-start | bytes 786440 | tf_op jit(solution)/shard_map/while/body/eval_jaxpr/ppermute | solution.py:46
  17.9 6.1 %collective-permute-start = (f32[512,128]{1,0:T(8,128)S(1)}, f32[512,128]{1,0:T(8,128)S(1)}, u32[]{:S(2)}, u32[]{:S(2)}) collective-permute-start(f32[512,128]{1,0:T(8,128)S(1)} %get-tuple-element.291), channel_id=1, source_target_pairs={{0,15},{1,0},{2,1},{3,2},{4,3},{5,4},{6,5},{7,6},{8,7},{9,8},{10,9... | collective-permute-start | bytes 786440 | tf_op jit(solution)/shard_map/while/body/eval_jaxpr/ppermute | solution.py:46
  28.0 7.1 %collective-permute-start = (f32[512,128]{1,0:T(8,128)S(1)}, f32[512,128]{1,0:T(8,128)S(1)}, u32[]{:S(2)}, u32[]{:S(2)}) collective-permute-start(f32[512,128]{1,0:T(8,128)S(1)} %get-tuple-element.291), channel_id=1, source_target_pairs={{0,15},{1,0},{2,1},{3,2},{4,3},{5,4},{6,5},{7,6},{8,7},{9,8},{10,9... | collective-permute-start | bytes 786440 | tf_op jit(solution)/shard_map/while/body/eval_jaxpr/ppermute | solution.py:46
  39.1 7.1 %collective-permute-start = (f32[512,128]{1,0:T(8,128)S(1)}, f32[512,128]{1,0:T(8,128)S(1)}, u32[]{:S(2)}, u32[]{:S(2)}) collective-permute-start(f32[512,128]{1,0:T(8,128)S(1)} %get-tuple-element.291), channel_id=1, source_target_pairs={{0,15},{1,0},{2,1},{3,2},{4,3},{5,4},{6,5},{7,6},{8,7},{9,8},{10,9... | collective-permute-start | bytes 786440 | tf_op jit(solution)/shard_map/while/body/eval_jaxpr/ppermute | solution.py:46
  50.1 7.1 %collective-permute-start = (f32[512,128]{1,0:T(8,128)S(1)}, f32[512,128]{1,0:T(8,128)S(1)}, u32[]{:S(2)}, u32[]{:S(2)}) collective-permute-start(f32[512,128]{1,0:T(8,128)S(1)} %get-tuple-element.291), channel_id=1, source_target_pairs={{0,15},{1,0},{2,1},{3,2},{4,3},{5,4},{6,5},{7,6},{8,7},{9,8},{10,9... | collective-permute-start | bytes 786440 | tf_op jit(solution)/shard_map/while/body/eval_jaxpr/ppermute | solution.py:46
  61.2 7.1 %collective-permute-start = (f32[512,128]{1,0:T(8,128)S(1)}, f32[512,128]{1,0:T(8,128)S(1)}, u32[]{:S(2)}, u32[]{:S(2)}) collective-permute-start(f32[512,128]{1,0:T(8,128)S(1)} %get-tuple-element.291), channel_id=1, source_target_pairs={{0,15},{1,0},{2,1},{3,2},{4,3},{5,4},{6,5},{7,6},{8,7},{9,8},{10,9... | collective-permute-start | bytes 786440 | tf_op jit(solution)/shard_map/while/body/eval_jaxpr/ppermute | solution.py:46
  72.3 7.1 %collective-permute-start = (f32[512,128]{1,0:T(8,128)S(1)}, f32[512,128]{1,0:T(8,128)S(1)}, u32[]{:S(2)}, u32[]{:S(2)}) collective-permute-start(f32[512,128]{1,0:T(8,128)S(1)} %get-tuple-element.291), channel_id=1, source_target_pairs={{0,15},{1,0},{2,1},{3,2},{4,3},{5,4},{6,5},{7,6},{8,7},{9,8},{10,9... | collective-permute-start | bytes 786440 | tf_op jit(solution)/shard_map/while/body/eval_jaxpr/ppermute | solution.py:46
  83.4 7.1 %collective-permute-start = (f32[512,128]{1,0:T(8,128)S(1)}, f32[512,128]{1,0:T(8,128)S(1)}, u32[]{:S(2)}, u32[]{:S(2)}) collective-permute-start(f32[512,128]{1,0:T(8,128)S(1)} %get-tuple-element.291), channel_id=1, source_target_pairs={{0,15},{1,0},{2,1},{3,2},{4,3},{5,4},{6,5},{7,6},{8,7},{9,8},{10,9... | collective-permute-start | bytes 786440 | tf_op jit(solution)/shard_map/while/body/eval_jaxpr/ppermute | solution.py:46
  94.5 7.1 %collective-permute-start = (f32[512,128]{1,0:T(8,128)S(1)}, f32[512,128]{1,0:T(8,128)S(1)}, u32[]{:S(2)}, u32[]{:S(2)}) collective-permute-start(f32[512,128]{1,0:T(8,128)S(1)} %get-tuple-element.291), channel_id=1, source_target_pairs={{0,15},{1,0},{2,1},{3,2},{4,3},{5,4},{6,5},{7,6},{8,7},{9,8},{10,9... | collective-permute-start | bytes 786440 | tf_op jit(solution)/shard_map/while/body/eval_jaxpr/ppermute | solution.py:46
  105.6 7.1 %collective-permute-start = (f32[512,128]{1,0:T(8,128)S(1)}, f32[512,128]{1,0:T(8,128)S(1)}, u32[]{:S(2)}, u32[]{:S(2)}) collective-permute-start(f32[512,128]{1,0:T(8,128)S(1)} %get-tuple-element.291), channel_id=1, source_target_pairs={{0,15},{1,0},{2,1},{3,2},{4,3},{5,4},{6,5},{7,6},{8,7},{9,8},{10,9... | collective-permute-start | bytes 786440 | tf_op jit(solution)/shard_map/while/body/eval_jaxpr/ppermute | solution.py:46
  116.6 7.1 %collective-permute-start = (f32[512,128]{1,0:T(8,128)S(1)}, f32[512,128]{1,0:T(8,128)S(1)}, u32[]{:S(2)}, u32[]{:S(2)}) collective-permute-start(f32[512,128]{1,0:T(8,128)S(1)} %get-tuple-element.291), channel_id=1, source_target_pairs={{0,15},{1,0},{2,1},{3,2},{4,3},{5,4},{6,5},{7,6},{8,7},{9,8},{10,9... | collective-permute-start | bytes 786440 | tf_op jit(solution)/shard_map/while/body/eval_jaxpr/ppermute | solution.py:46
  127.7 7.1 %collective-permute-start = (f32[512,128]{1,0:T(8,128)S(1)}, f32[512,128]{1,0:T(8,128)S(1)}, u32[]{:S(2)}, u32[]{:S(2)}) collective-permute-start(f32[512,128]{1,0:T(8,128)S(1)} %get-tuple-element.291), channel_id=1, source_target_pairs={{0,15},{1,0},{2,1},{3,2},{4,3},{5,4},{6,5},{7,6},{8,7},{9,8},{10,9... | collective-permute-start | bytes 786440 | tf_op jit(solution)/shard_map/while/body/eval_jaxpr/ppermute | solution.py:46
  138.8 7.1 %collective-permute-start = (f32[512,128]{1,0:T(8,128)S(1)}, f32[512,128]{1,0:T(8,128)S(1)}, u32[]{:S(2)}, u32[]{:S(2)}) collective-permute-start(f32[512,128]{1,0:T(8,128)S(1)} %get-tuple-element.291), channel_id=1, source_target_pairs={{0,15},{1,0},{2,1},{3,2},{4,3},{5,4},{6,5},{7,6},{8,7},{9,8},{10,9... | collective-permute-start | bytes 786440 | tf_op jit(solution)/shard_map/while/body/eval_jaxpr/ppermute | solution.py:46
  149.9 7.1 %collective-permute-start = (f32[512,128]{1,0:T(8,128)S(1)}, f32[512,128]{1,0:T(8,128)S(1)}, u32[]{:S(2)}, u32[]{:S(2)}) collective-permute-start(f32[512,128]{1,0:T(8,128)S(1)} %get-tuple-element.291), channel_id=1, source_target_pairs={{0,15},{1,0},{2,1},{3,2},{4,3},{5,4},{6,5},{7,6},{8,7},{9,8},{10,9... | collective-permute-start | bytes 786440 | tf_op jit(solution)/shard_map/while/body/eval_jaxpr/ppermute | solution.py:46
  161.0 7.1 %collective-permute-start = (f32[512,128]{1,0:T(8,128)S(1)}, f32[512,128]{1,0:T(8,128)S(1)}, u32[]{:S(2)}, u32[]{:S(2)}) collective-permute-start(f32[512,128]{1,0:T(8,128)S(1)} %get-tuple-element.291), channel_id=1, source_target_pairs={{0,15},{1,0},{2,1},{3,2},{4,3},{5,4},{6,5},{7,6},{8,7},{9,8},{10,9... | collective-permute-start | bytes 786440 | tf_op jit(solution)/shard_map/while/body/eval_jaxpr/ppermute | solution.py:46
  172.1 7.1 %collective-permute-start = (f32[512,128]{1,0:T(8,128)S(1)}, f32[512,128]{1,0:T(8,128)S(1)}, u32[]{:S(2)}, u32[]{:S(2)}) collective-permute-start(f32[512,128]{1,0:T(8,128)S(1)} %get-tuple-element.291), channel_id=1, source_target_pairs={{0,15},{1,0},{2,1},{3,2},{4,3},{5,4},{6,5},{7,6},{8,7},{9,8},{10,9... | collective-permute-start | bytes 786440 | tf_op jit(solution)/shard_map/while/body/eval_jaxpr/ppermute | solution.py:46
  183.1 7.1 %collective-permute-start = (f32[512,128]{1,0:T(8,128)S(1)}, f32[512,128]{1,0:T(8,128)S(1)}, u32[]{:S(2)}, u32[]{:S(2)}) collective-permute-start(f32[512,128]{1,0:T(8,128)S(1)} %get-tuple-element.291), channel_id=1, source_target_pairs={{0,15},{1,0},{2,1},{3,2},{4,3},{5,4},{6,5},{7,6},{8,7},{9,8},{10,9... | collective-permute-start | bytes 786440 | tf_op jit(solution)/shard_map/while/body/eval_jaxpr/ppermute | solution.py:46
  194.2 7.1 %collective-permute-start = (f32[512,128]{1,0:T(8,128)S(1)}, f32[512,128]{1,0:T(8,128)S(1)}, u32[]{:S(2)}, u32[]{:S(2)}) collective-permute-start(f32[512,128]{1,0:T(8,128)S(1)} %get-tuple-element.291), channel_id=1, source_target_pairs={{0,15},{1,0},{2,1},{3,2},{4,3},{5,4},{6,5},{7,6},{8,7},{9,8},{10,9... | collective-permute-start | bytes 786440 | tf_op jit(solution)/shard_map/while/body/eval_jaxpr/ppermute | solution.py:46
  205.3 7.1 %collective-permute-start = (f32[512,128]{1,0:T(8,128)S(1)}, f32[512,128]{1,0:T(8,128)S(1)}, u32[]{:S(2)}, u32[]{:S(2)}) collective-permute-start(f32[512,128]{1,0:T(8,128)S(1)} %get-tuple-element.291), channel_id=1, source_target_pairs={{0,15},{1,0},{2,1},{3,2},{4,3},{5,4},{6,5},{7,6},{8,7},{9,8},{10,9... | collective-permute-start | bytes 786440 | tf_op jit(solution)/shard_map/while/body/eval_jaxpr/ppermute | solution.py:46
  216.4 7.1 %collective-permute-start = (f32[512,128]{1,0:T(8,128)S(1)}, f32[512,128]{1,0:T(8,128)S(1)}, u32[]{:S(2)}, u32[]{:S(2)}) collective-permute-start(f32[512,128]{1,0:T(8,128)S(1)} %get-tuple-element.291), channel_id=1, source_target_pairs={{0,15},{1,0},{2,1},{3,2},{4,3},{5,4},{6,5},{7,6},{8,7},{9,8},{10,9... | collective-permute-start | bytes 786440 | tf_op jit(solution)/shard_map/while/body/eval_jaxpr/ppermute | solution.py:46
  227.5 7.1 %collective-permute-start = (f32[512,128]{1,0:T(8,128)S(1)}, f32[512,128]{1,0:T(8,128)S(1)}, u32[]{:S(2)}, u32[]{:S(2)}) collective-permute-start(f32[512,128]{1,0:T(8,128)S(1)} %get-tuple-element.291), channel_id=1, source_target_pairs={{0,15},{1,0},{2,1},{3,2},{4,3},{5,4},{6,5},{7,6},{8,7},{9,8},{10,9... | collective-permute-start | bytes 786440 | tf_op jit(solution)/shard_map/while/body/eval_jaxpr/ppermute | solution.py:46
  238.5 7.1 %collective-permute-start = (f32[512,128]{1,0:T(8,128)S(1)}, f32[512,128]{1,0:T(8,128)S(1)}, u32[]{:S(2)}, u32[]{:S(2)}) collective-permute-start(f32[512,128]{1,0:T(8,128)S(1)} %get-tuple-element.291), channel_id=1, source_target_pairs={{0,15},{1,0},{2,1},{3,2},{4,3},{5,4},{6,5},{7,6},{8,7},{9,8},{10,9... | collective-permute-start | bytes 786440 | tf_op jit(solution)/shard_map/while/body/eval_jaxpr/ppermute | solution.py:46
  249.6 7.1 %collective-permute-start = (f32[512,128]{1,0:T(8,128)S(1)}, f32[512,128]{1,0:T(8,128)S(1)}, u32[]{:S(2)}, u32[]{:S(2)}) collective-permute-start(f32[512,128]{1,0:T(8,128)S(1)} %get-tuple-element.291), channel_id=1, source_target_pairs={{0,15},{1,0},{2,1},{3,2},{4,3},{5,4},{6,5},{7,6},{8,7},{9,8},{10,9... | collective-permute-start | bytes 786440 | tf_op jit(solution)/shard_map/while/body/eval_jaxpr/ppermute | solution.py:46
  260.7 7.1 %collective-permute-start = (f32[512,128]{1,0:T(8,128)S(1)}, f32[512,128]{1,0:T(8,128)S(1)}, u32[]{:S(2)}, u32[]{:S(2)}) collective-permute-start(f32[512,128]{1,0:T(8,128)S(1)} %get-tuple-element.291), channel_id=1, source_target_pairs={{0,15},{1,0},{2,1},{3,2},{4,3},{5,4},{6,5},{7,6},{8,7},{9,8},{10,9... | collective-permute-start | bytes 786440 | tf_op jit(solution)/shard_map/while/body/eval_jaxpr/ppermute | solution.py:46
  271.8 7.1 %collective-permute-start = (f32[512,128]{1,0:T(8,128)S(1)}, f32[512,128]{1,0:T(8,128)S(1)}, u32[]{:S(2)}, u32[]{:S(2)}) collective-permute-start(f32[512,128]{1,0:T(8,128)S(1)} %get-tuple-element.291), channel_id=1, source_target_pairs={{0,15},{1,0},{2,1},{3,2},{4,3},{5,4},{6,5},{7,6},{8,7},{9,8},{10,9... | collective-permute-start | bytes 786440 | tf_op jit(solution)/shard_map/while/body/eval_jaxpr/ppermute | solution.py:46
  282.9 7.1 %collective-permute-start = (f32[512,128]{1,0:T(8,128)S(1)}, f32[512,128]{1,0:T(8,128)S(1)}, u32[]{:S(2)}, u32[]{:S(2)}) collective-permute-start(f32[512,128]{1,0:T(8,128)S(1)} %get-tuple-element.291), channel_id=1, source_target_pairs={{0,15},{1,0},{2,1},{3,2},{4,3},{5,4},{6,5},{7,6},{8,7},{9,8},{10,9... | collective-permute-start | bytes 786440 | tf_op jit(solution)/shard_map/while/body/eval_jaxpr/ppermute | solution.py:46
  294.0 7.1 %collective-permute-start = (f32[512,128]{1,0:T(8,128)S(1)}, f32[512,128]{1,0:T(8,128)S(1)}, u32[]{:S(2)}, u32[]{:S(2)}) collective-permute-start(f32[512,128]{1,0:T(8,128)S(1)} %get-tuple-element.291), channel_id=1, source_target_pairs={{0,15},{1,0},{2,1},{3,2},{4,3},{5,4},{6,5},{7,6},{8,7},{9,8},{10,9... | collective-permute-start | bytes 786440 | tf_op jit(solution)/shard_map/while/body/eval_jaxpr/ppermute | solution.py:46
  305.0 7.1 %collective-permute-start = (f32[512,128]{1,0:T(8,128)S(1)}, f32[512,128]{1,0:T(8,128)S(1)}, u32[]{:S(2)}, u32[]{:S(2)}) collective-permute-start(f32[512,128]{1,0:T(8,128)S(1)} %get-tuple-element.291), channel_id=1, source_target_pairs={{0,15},{1,0},{2,1},{3,2},{4,3},{5,4},{6,5},{7,6},{8,7},{9,8},{10,9... | collective-permute-start | bytes 786440 | tf_op jit(solution)/shard_map/while/body/eval_jaxpr/ppermute | solution.py:46
  316.1 7.1 %collective-permute-start = (f32[512,128]{1,0:T(8,128)S(1)}, f32[512,128]{1,0:T(8,128)S(1)}, u32[]{:S(2)}, u32[]{:S(2)}) collective-permute-start(f32[512,128]{1,0:T(8,128)S(1)} %get-tuple-element.291), channel_id=1, source_target_pairs={{0,15},{1,0},{2,1},{3,2},{4,3},{5,4},{6,5},{7,6},{8,7},{9,8},{10,9... | collective-permute-start | bytes 786440 | tf_op jit(solution)/shard_map/while/body/eval_jaxpr/ppermute | solution.py:46
  327.2 7.1 %collective-permute-start = (f32[512,128]{1,0:T(8,128)S(1)}, f32[512,128]{1,0:T(8,128)S(1)}, u32[]{:S(2)}, u32[]{:S(2)}) collective-permute-start(f32[512,128]{1,0:T(8,128)S(1)} %get-tuple-element.291), channel_id=1, source_target_pairs={{0,15},{1,0},{2,1},{3,2},{4,3},{5,4},{6,5},{7,6},{8,7},{9,8},{10,9... | collective-permute-start | bytes 786440 | tf_op jit(solution)/shard_map/while/body/eval_jaxpr/ppermute | solution.py:46
  338.3 7.1 %collective-permute-start = (f32[512,128]{1,0:T(8,128)S(1)}, f32[512,128]{1,0:T(8,128)S(1)}, u32[]{:S(2)}, u32[]{:S(2)}) collective-permute-start(f32[512,128]{1,0:T(8,128)S(1)} %get-tuple-element.291), channel_id=1, source_target_pairs={{0,15},{1,0},{2,1},{3,2},{4,3},{5,4},{6,5},{7,6},{8,7},{9,8},{10,9... | collective-permute-start | bytes 786440 | tf_op jit(solution)/shard_map/while/body/eval_jaxpr/ppermute | solution.py:46
  349.4 7.1 %collective-permute-start = (f32[512,128]{1,0:T(8,128)S(1)}, f32[512,128]{1,0:T(8,128)S(1)}, u32[]{:S(2)}, u32[]{:S(2)}) collective-permute-start(f32[512,128]{1,0:T(8,128)S(1)} %get-tuple-element.291), channel_id=1, source_target_pairs={{0,15},{1,0},{2,1},{3,2},{4,3},{5,4},{6,5},{7,6},{8,7},{9,8},{10,9... | collective-permute-start | bytes 786440 | tf_op jit(solution)/shard_map/while/body/eval_jaxpr/ppermute | solution.py:46
  (4 other events, 5.3 us)
where the time goes:
time: 362 us; the launch traced here: 357 us
  starting transfers between devices  186 us (51%)
  matrix products  87.7 us (24%)
  waiting for transfers between devices  38.6 us (11%)
  local copies, waits for them, and re-layouts  34 us (9%)
  loops' own time  7.86 us (2%)
    ppermute x32, starting transfers between devices, stratum(): item_blk = lax.ppermute(item_blk, 'shard', shift_back)  186 us
    dot_general x128, matrix products, step(): jnp.einsum('ui,ur->ir', residual, user_bf, preferred_element_type=jnp.flo...  50 us
    ppermute x32, waiting for transfers between devices, stratum(): item_blk = lax.ppermute(item_blk, 'shard', shift_back)  38.6 us
    dot_general x128, matrix products, step(): grad_user = jnp.dot(residual, item_bf, preferred_element_type=jnp.float32)  37.7 us
    dynamic_slice x32, local copies, waits for them, and re-layouts, stratum(): rating_blk = lax.dynamic_slice_in_dim(ratings, col_start, items_dev, axis=1)  29.5 us
  transfers between devices with their start and end apart: 32, of which 32 were waited for; matrix products, arithmetic and copies ran while one was open for 0% of the time, Pallas kernels for 0%

commit v1 on v0

v1 whole, which is shorter than its diff:
```python
import functools
import math

import jax
import jax.numpy as jnp
from jax import lax
from jax.experimental import pallas as pl
from jax.experimental.pallas import tpu as pltpu
from jax.sharding import PartitionSpec as P

STRATUM_STEPS = 4
EPOCHS = 2
QUAD = 4
AHEAD = 4
MESH = pl.DeviceIdType.MESH


def kernel(
    n, step_size, weight_decay, ratings, observed, user_in, item_in, user_out, item_out,
    rate_stage, seen_stage, code_send, code, items, users, items_bf,
    load_r, load_m, code_ss, code_rs, user_ss, user_rs, item_ss, item_rs,
):
    n_rows, rank = user_in.shape
    n_items = item_in.shape[0]
    strata = EPOCHS * n
    me = lax.axis_index("shard")
    lane = lax.rem(me, QUAD)
    base = me - lane
    ahead_dev = lax.rem(me + QUAD, n)
    back_dev = lax.rem(me + n - QUAD, n)

    def mate(offset):
        return base + lax.rem(lane + offset, QUAD)

    def loads(t):
        col = pl.multiple_of(lax.rem(me + t, n) * n_items, n_items)
        return (
            pltpu.make_async_copy(ratings.at[:, pl.ds(col, n_items)], rate_stage.at[t], load_r.at[t]),
            pltpu.make_async_copy(observed.at[:, pl.ds(col, n_items)], seen_stage.at[t], load_m.at[t]),
        )

    def code_copy(t, offset):
        return pltpu.make_async_remote_copy(
            src_ref=code_send.at[t], dst_ref=code.at[t], send_sem=code_ss.at[t], recv_sem=code_rs.at[t],
            device_id={"shard": mate(offset)}, device_id_type=MESH)

    def user_copy(t):
        return pltpu.make_async_remote_copy(
            src_ref=users.at[t], dst_ref=users.at[t + 1], send_sem=user_ss.at[t], recv_sem=user_rs.at[t],
            device_id={"shard": mate(1)}, device_id_type=MESH)

    def item_copy(k):
        return pltpu.make_async_remote_copy(
            src_ref=items.at[k], dst_ref=items.at[k + 1], send_sem=item_ss.at[k], recv_sem=item_rs.at[k],
            device_id={"shard": back_dev}, device_id_type=MESH)

    def coded(t):
        return jnp.where(seen_stage[t] != 0, rate_stage[t], jnp.inf)

    def make_code(t, offset):
        for load in loads(t):
            load.wait()
        if offset == 0:
            code[t] = coded(t)
        else:
            code_send[t] = coded(t)
            code_copy(t, offset).start()

    @pl.loop(0, n)
    def _(t):
        for load in loads(t):
            load.start()

    barrier = pltpu.get_barrier_semaphore()
    greeted = [mate(1), mate(2), mate(3), ahead_dev, back_dev]
    for dev in greeted:
        pl.semaphore_signal(barrier, inc=1, device_id={"shard": dev}, device_id_type=MESH)

    users[0] = user_in[...]
    items[0] = item_in[...].T
    items_bf[...] = items[0].astype(jnp.bfloat16)
    pl.semaphore_wait(barrier, len(greeted))
    for t in range(AHEAD):
        make_code(t, t % QUAD)

    def stratum(t, offset, coding):
        turns = (t - lane + QUAD - 1) // QUAD
        first = lax.rem(lane + QUAD - offset, QUAD) == QUAD - 1
        last = lax.rem(lane + QUAD - offset, QUAD) == 0

        @pl.when(jnp.logical_and(first, t > 0))
        def _():
            item_copy(turns - 1).wait_recv()
            items_bf[...] = items[turns].astype(jnp.bfloat16)

        if coding:
            make_code(t + AHEAD, (offset + AHEAD) % QUAD)
            if offset != 0:
                code_copy(t, offset).wait_recv()

        @pl.when(t > 0)
        def _():
            user_copy(t - 1).wait_recv()

        user = users[t]
        user_bf = user.astype(jnp.bfloat16)
        for step in range(STRATUM_STEPS):
            pred = jnp.dot(user_bf, items_bf[...], preferred_element_type=jnp.float32)
            rate = code[lax.rem(t, n)]
            err = jnp.where(rate < jnp.inf, pred - rate, 0.0).astype(jnp.bfloat16)
            grad = lax.dot_general(err, items_bf[...], (((1,), (1,)), ((), ())), preferred_element_type=jnp.float32)
            user = user - step_size * (grad + weight_decay * user)
            user_bf = user.astype(jnp.bfloat16)
            if step == STRATUM_STEPS - 1:
                users[t] = user
                user_copy(t).start()
            pred = jnp.dot(user_bf, items_bf[...], preferred_element_type=jnp.float32)
            rate = code[lax.rem(t, n)]
            err = jnp.where(rate < jnp.inf, pred - rate, 0.0).astype(jnp.bfloat16)
            grad = lax.dot_general(user_bf, err, (((0,), (0,)), ((), ())), preferred_element_type=jnp.float32)
            item = items[turns]
            item = item - step_size * (grad + weight_decay * item)
            items[turns] = item
            items_bf[...] = item.astype(jnp.bfloat16)

        @pl.when(last)
        def _():
            item_copy(turns).start()

    @pl.loop(0, (n - AHEAD) // QUAD)
    def _(rnd):
        for offset in range(QUAD):
            stratum(rnd * QUAD + offset, offset, True)

    @pl.loop((n - AHEAD) // QUAD, strata // QUAD)
    def _(rnd):
        for offset in range(QUAD):
            t = rnd * QUAD + offset
            if offset != 0:
                @pl.when(t < n)
                def _():
                    code_copy(t, offset).wait_recv()
            stratum(t, offset, False)

    shifts = strata // QUAD

    @pl.when(lane == QUAD - 1)
    def _():
        item_copy(shifts - 1).wait_recv()

    item_out[...] = items[shifts]
    user_copy(strata - 1).wait_recv()
    user_out[...] = users[strata]

    @pl.loop(0, strata)
    def _(t):
        user_copy(t).wait_send()

    @pl.loop(0, shifts)
    def _(k):
        item_copy(k).wait_send()

    @pl.loop(0, n // QUAD)
    def _(rnd):
        for offset in range(1, QUAD):
            code_copy(rnd * QUAD + offset, offset).wait_send()


def solution(mesh):
    n = mesh.shape["shard"]
    row_spec = P(("rep", "shard"), None)

    def local(ratings, observed, user_init, item_init):
        users_dev = ratings.shape[0]
        items_dev, rank = item_init.shape
        step_size = 0.5 / ((users_dev + items_dev + rank) / math.sqrt(rank))
        weight_decay = 0.03 * math.sqrt(users_dev * items_dev / rank)
        strata = EPOCHS * n
        shifts = strata // QUAD
        vmem = pl.BlockSpec(memory_space=pltpu.VMEM)
        anywhere = pl.BlockSpec(memory_space=pl.ANY)
        dma = pltpu.SemaphoreType.DMA
        user_out, item_out = pl.pallas_call(
            functools.partial(kernel, n, step_size, weight_decay),
            out_shape=(
                jax.ShapeDtypeStruct((users_dev, rank), jnp.float32),
                jax.ShapeDtypeStruct((rank, items_dev), jnp.float32),
            ),
            in_specs=[anywhere, anywhere, vmem, vmem],
            out_specs=(vmem, vmem),
            scratch_shapes=[
                pltpu.VMEM((n, users_dev, items_dev), jnp.float32),
                pltpu.VMEM((n, users_dev, items_dev), jnp.int32),
                pltpu.VMEM((n, users_dev, items_dev), jnp.float32),
                pltpu.VMEM((n, users_dev, items_dev), jnp.float32),
                pltpu.VMEM((shifts + 1, rank, items_dev), jnp.float32),
                pltpu.VMEM((strata + 1, users_dev, rank), jnp.float32),
                pltpu.VMEM((rank, items_dev), jnp.bfloat16),
                dma((n,)), dma((n,)), dma((n,)), dma((n,)),
                dma((strata,)), dma((strata,)), dma((shifts,)), dma((shifts,)),
            ],
            compiler_params=pltpu.CompilerParams(collective_id=0, has_side_effects=True),
        )(ratings, observed, user_init, item_init)
        return user_out, item_out.T

    return jax.shard_map(local, mesh=mesh, in_specs=(row_spec,) * 4, out_specs=(row_spec, row_spec), check_vma=False)
```

time: 362 us -> 174 us (0.48); the launches traced: 357 us -> 173 us
  starting transfers between devices: 186 us -> 0 us
  Pallas kernels: 0 us -> 170 us
  matrix products: 87.7 us -> 0 us
  waiting for transfers between devices: 38.6 us -> 0 us
  local copies, waits for them, and re-layouts: 34 us -> 3.16 us
  loops' own time: 7.86 us -> 0 us
    ppermute x32 -> x0, starting transfers between devices: 186 us -> none  [stratum(): item_blk = lax.ppermute(item_blk, 'shard', shift_back)]
    pallas_call x0 -> x1, Pallas kernels: none -> 170 us  [local(): pl.pallas_call(functools.partial(kernel, n, step_size, weight_decay), out...]
    dot_general x256 -> x0, matrix products: 87.7 us -> none  [the longest x128 50 us: step(): jnp.einsum('ui,ur->ir', residual, user_bf, preferred_element_type=jnp.flo...]
    ppermute x32 -> x0, waiting for transfers between devices: 38.6 us -> none  [stratum(): item_blk = lax.ppermute(item_blk, 'shard', shift_back)]
    dynamic_slice x64 -> x0, local copies, waits for them, and re-layouts: 29.8 us -> none  [the longest x32 29.5 us: stratum(): rating_blk = lax.dynamic_slice_in_dim(ratings, col_start, items_dev, axis=1)]
    another operation x33 -> x0, loops' own time: 7.86 us -> none  [the longest x32 5.89 us: stratum(): lax.fori_loop(0, STRATUM_STEPS, step, (user_blk, item_blk))]
  transfers between devices with their start and end apart: 32 -> 0, of which waited for: 32 -> 0; matrix products, arithmetic and copies ran while one was open for 0% -> 0% of each run, Pallas kernels for 0% -> 0%
where the time goes in v1:
time: 174 us; the launch traced here: 173 us
  Pallas kernels  170 us (98%)
  local copies, waits for them, and re-layouts  3.16 us (2%)
    pallas_call x1, Pallas kernels, local(): pl.pallas_call(functools.partial(kernel, n, step_size, weight_decay), out...  170 us

profile of v1, /device:TPU:21, one launch (start us, length us, event | category | flops | bytes accessed | tf_op | source)
XLA Modules:
  0.0 173.4 jit_solution(7876633908528559969)
XLA Ops:
  0.6 169.6 %shard_map.59 = (f32[64,128]{1,0:T(8,128)}, f32[128,512]{1,0:T(8,128)}) custom-call(f32[64,8192]{1,0:T(8,128)} %ratings.1, s32[64,8192]{1,0:T(8,128)} %observed.1, f32[64,128]{1,0:T(8,128)} %user_in.1, f32[512,128]{1,0:T(8,128)} %item_in.1), custom_call_target="tpu_custom_call" | custom-call | tf_op jit(solution)/shard_map/pallas_call | solution.py:183
  170.2 1.8 %copy.6 = f32[512,128]{1,0:T(8,128)} copy(f32[512,128]{0,1:T(8,128)} %bitcast.1) | data formatting | bytes 524288
  172.0 1.4 copy.8

commit v2 on v1

v2 whole, which is shorter than its diff:
```python
import functools
import math

import jax
import jax.numpy as jnp
from jax import lax
from jax.experimental import pallas as pl
from jax.experimental.pallas import tpu as pltpu
from jax.sharding import PartitionSpec as P

STRATUM_STEPS = 4
EPOCHS = 2
AHEAD = 2
AHEAD_DOWN = 4
MESH = pl.DeviceIdType.MESH


def kernel(
    n, step_size, weight_decay, ratings, observed, user_in, item_in, user_out, item_out,
    rate_stage, seen_stage, code_send, code, items, items_bf, users,
    load_r, load_m, code_ss, code_rs, user_ss, user_rs,
):
    n_items = item_in.shape[0]
    strata = EPOCHS * n
    half = n // 2
    me = lax.axis_index("shard")

    def up(offset):
        return {"shard": lax.rem(me + offset, n)}

    def loads(t):
        col = pl.multiple_of(lax.rem(me + t, n) * n_items, n_items)
        return (
            pltpu.make_async_copy(ratings.at[:, pl.ds(col, n_items)], rate_stage.at[t], load_r.at[t]),
            pltpu.make_async_copy(observed.at[:, pl.ds(col, n_items)], seen_stage.at[t], load_m.at[t]),
        )

    def code_copy(t):
        return pltpu.make_async_remote_copy(
            src_ref=code_send.at[t], dst_ref=code.at[t], send_sem=code_ss.at[t], recv_sem=code_rs.at[t],
            device_id=up(t), device_id_type=MESH)

    def user_copy(t):
        return pltpu.make_async_remote_copy(
            src_ref=users.at[t], dst_ref=users.at[t + 1], send_sem=user_ss.at[t], recv_sem=user_rs.at[t],
            device_id=up(1), device_id_type=MESH)

    def coded(t):
        for load in loads(t):
            load.wait()
        return jnp.where(seen_stage[t] != 0, rate_stage[t], jnp.inf)

    def send_code(t):
        code_send[t] = coded(t)
        code_copy(t).start()

    @pl.loop(0, n)
    def _(t):
        for load in loads(t):
            load.start()

    barrier = pltpu.get_barrier_semaphore()
    for offset in range(1, n):
        pl.semaphore_signal(barrier, inc=1, device_id=up(offset), device_id_type=MESH)

    users[0] = user_in[...]
    items[...] = item_in[...].T
    items_bf[...] = items[...].astype(jnp.bfloat16)
    code[0] = coded(0)
    pl.semaphore_wait(barrier, n - 1)
    for t in range(1, AHEAD):
        send_code(t)

    @pl.loop(0, strata)
    def _(t):
        @pl.when(t + AHEAD <= half)
        def _():
            send_code(t + AHEAD)

        @pl.when(jnp.logical_and(t + AHEAD_DOWN > half, t + AHEAD_DOWN < n))
        def _():
            send_code(t + AHEAD_DOWN)

        @pl.when(jnp.logical_and(t > 0, t < n))
        def _():
            code_copy(t).wait_recv()

        @pl.when(t > 0)
        def _():
            user_copy(t - 1).wait_recv()

        slot = lax.rem(t, n)
        user = users[t]
        user_bf = user.astype(jnp.bfloat16)
        for step in range(STRATUM_STEPS):
            pred = jnp.dot(user_bf, items_bf[...], preferred_element_type=jnp.float32)
            rate = code[slot]
            err = jnp.where(rate < jnp.inf, pred - rate, 0.0).astype(jnp.bfloat16)
            grad = lax.dot_general(err, items_bf[...], (((1,), (1,)), ((), ())), preferred_element_type=jnp.float32)
            user = user - step_size * (grad + weight_decay * user)
            user_bf = user.astype(jnp.bfloat16)
            if step == STRATUM_STEPS - 1:
                users[t] = user
                user_copy(t).start()
            pred = jnp.dot(user_bf, items_bf[...], preferred_element_type=jnp.float32)
            rate = code[slot]
            err = jnp.where(rate < jnp.inf, pred - rate, 0.0).astype(jnp.bfloat16)
            grad = lax.dot_general(user_bf, err, (((0,), (0,)), ((), ())), preferred_element_type=jnp.float32)
            item = items[...]
            item = item - step_size * (grad + weight_decay * item)
            items[...] = item
            items_bf[...] = item.astype(jnp.bfloat16)

    item_out[...] = items[...]
    user_copy(strata - 1).wait_recv()
    user_out[...] = users[strata]

    @pl.loop(0, strata)
    def _(t):
        user_copy(t).wait_send()

    @pl.loop(1, n)
    def _(t):
        code_copy(t).wait_send()


def solution(mesh):
    n = mesh.shape["shard"]
    row_spec = P(("rep", "shard"), None)

    def local(ratings, observed, user_init, item_init):
        users_dev = ratings.shape[0]
        items_dev, rank = item_init.shape
        step_size = 0.5 / ((users_dev + items_dev + rank) / math.sqrt(rank))
        weight_decay = 0.03 * math.sqrt(users_dev * items_dev / rank)
        strata = EPOCHS * n
        vmem = pl.BlockSpec(memory_space=pltpu.VMEM)
        anywhere = pl.BlockSpec(memory_space=pl.ANY)
        dma = pltpu.SemaphoreType.DMA
        user_out, item_out = pl.pallas_call(
            functools.partial(kernel, n, step_size, weight_decay),
            out_shape=(
                jax.ShapeDtypeStruct((users_dev, rank), jnp.float32),
                jax.ShapeDtypeStruct((rank, items_dev), jnp.float32),
            ),
            in_specs=[anywhere, anywhere, vmem, vmem],
            out_specs=(vmem, vmem),
            scratch_shapes=[
                pltpu.VMEM((n, users_dev, items_dev), jnp.float32),
                pltpu.VMEM((n, users_dev, items_dev), jnp.int32),
                pltpu.VMEM((n, users_dev, items_dev), jnp.float32),
                pltpu.VMEM((n, users_dev, items_dev), jnp.float32),
                pltpu.VMEM((rank, items_dev), jnp.float32),
                pltpu.VMEM((rank, items_dev), jnp.bfloat16),
                pltpu.VMEM((strata + 1, users_dev, rank), jnp.float32),
                dma((n,)), dma((n,)), dma((n,)), dma((n,)), dma((strata,)), dma((strata,)),
            ],
            compiler_params=pltpu.CompilerParams(collective_id=0, has_side_effects=True),
        )(ratings, observed, user_init, item_init)
        return user_out, item_out.T

    return jax.shard_map(local, mesh=mesh, in_specs=(row_spec,) * 4, out_specs=(row_spec, row_spec), check_vma=False)
```

time: 174 us -> 160 us (0.920)
  Pallas kernels: 170 us -> 156 us
    pallas_call x1, Pallas kernels: 170 us -> 156 us  [local(): pl.pallas_call(functools.partial(kernel, n, step_size, weight_decay), out...]
where the time goes in v2:
time: 160 us
  Pallas kernels  156 us (98%)
  local copies, waits for them, and re-layouts  3.16 us (2%)
    pallas_call x1, Pallas kernels, local(): pl.pallas_call(functools.partial(kernel, n, step_size, weight_decay), out...  156 us

profile of v2, /device:TPU:21, one launch (start us, length us, event | category | flops | bytes accessed | tf_op | source)
XLA Modules:
  0.0 159.7 jit_solution(9310894596954396456)
XLA Ops:
  0.6 155.9 %shard_map.59 = (f32[64,128]{1,0:T(8,128)}, f32[128,512]{1,0:T(8,128)}) custom-call(f32[64,8192]{1,0:T(8,128)} %ratings.1, s32[64,8192]{1,0:T(8,128)} %observed.1, f32[64,128]{1,0:T(8,128)} %user_in.1, f32[512,128]{1,0:T(8,128)} %item_in.1), custom_call_target="tpu_custom_call" | custom-call | tf_op jit(solution)/shard_map/pallas_call | solution.py:140
  156.5 1.8 %copy.6 = f32[512,128]{1,0:T(8,128)} copy(f32[512,128]{0,1:T(8,128)} %bitcast.1) | data formatting | bytes 524288
  158.3 1.4 copy.8

commit v3 on v2

v3 whole, which is shorter than its diff:
```python
import functools
import math

import jax
import jax.numpy as jnp
from jax import lax
from jax.experimental import pallas as pl
from jax.experimental.pallas import tpu as pltpu
from jax.sharding import PartitionSpec as P

STRATUM_STEPS = 4
EPOCHS = 2
CORES = 2
RELAY_HOP = 4
SEND_AT = {1: 0, 2: 0, 3: 1, 4: 3, 5: 2, 6: 4, 7: 0, 8: 0, 9: 4, 10: 1, 11: 7, 12: 8, 13: 9, 14: 13, 15: 12, 16: 14}
RELAY_AT = {7: 1, 8: 2}
MESH = pl.DeviceIdType.MESH


def kernel(
    n, step_size, weight_decay, ratings, observed, user_in, item_in, user_out, item_out,
    rate_stage, seen_stage, code_send, code, relay, item_stage, items, items_bf, users,
    load_r, load_m, load_i, load_u, code_ss, code_rs, relay_ss, relay_rs, user_ss, user_rs,
    item_ss, item_rs, bf_ss, bf_rs,
):
    n_items = item_in.shape[0]
    strata = EPOCHS * n
    chips = n // CORES
    me = lax.axis_index("shard")
    chip = me // CORES
    core = lax.rem(me, CORES)
    odd_chip = lax.rem(chip, 2)
    partner = me + 1 - 2 * core
    relayed = sorted(RELAY_AT)

    def at(device):
        return {"shard": device}

    def block_place(owner, b):
        item = lax.rem(owner + b, n)
        return item - lax.rem(item, 2) + lax.rem(owner + item // 2, 2)

    def loads(b):
        col = pl.multiple_of(lax.rem(me + b, n) * n_items, n_items)
        slot = b % n
        return (
            pltpu.make_async_copy(ratings.at[:, pl.ds(col, n_items)], rate_stage.at[slot], load_r.at[slot]),
            pltpu.make_async_copy(observed.at[:, pl.ds(col, n_items)], seen_stage.at[slot], load_m.at[slot]),
        )

    def code_copy(b):
        return pltpu.make_async_remote_copy(
            src_ref=code_send.at[b], dst_ref=code.at[b], send_sem=code_ss.at[b], recv_sem=code_rs.at[b],
            device_id=at(block_place(me, b)), device_id_type=MESH)

    def relay_in(b):
        r = relayed.index(b)
        return pltpu.make_async_remote_copy(
            src_ref=code_send.at[b], dst_ref=relay.at[r], send_sem=relay_ss.at[r], recv_sem=relay_rs.at[r],
            device_id=at(lax.rem(me + n - RELAY_HOP, n)), device_id_type=MESH)

    def relay_out(b):
        return pltpu.make_async_remote_copy(
            src_ref=relay.at[relayed.index(b)], dst_ref=code.at[b], send_sem=code_ss.at[b], recv_sem=code_rs.at[b],
            device_id=at(block_place(lax.rem(me + RELAY_HOP, n), b)), device_id_type=MESH)

    def user_copy(t, device):
        return pltpu.make_async_remote_copy(
            src_ref=users.at[t], dst_ref=users.at[t + 1], send_sem=user_ss.at[t], recv_sem=user_rs.at[t],
            device_id=at(device), device_id_type=MESH)

    def bf_copy(t):
        return pltpu.make_async_remote_copy(
            src_ref=items_bf.at[t], dst_ref=items_bf.at[t + 1], send_sem=bf_ss.at[t], recv_sem=bf_rs.at[t],
            device_id=at(partner), device_id_type=MESH)

    def item_copy(t):
        return pltpu.make_async_remote_copy(
            src_ref=items.at[t], dst_ref=items.at[t + 1], send_sem=item_ss.at[t], recv_sem=item_rs.at[t],
            device_id=at(partner), device_id_type=MESH)

    def item_half(t):
        if isinstance(t, int) and t in (0, strata):
            return core
        return lax.rem(core + t + chip, 2)

    def user_next(t):
        half = item_half(t)
        up = lax.rem(chip + half, chips)
        shift = t + 1
        if isinstance(t, int) and t + 1 == strata:
            return CORES * up + lax.rem(1 - half + shift, 2)
        return CORES * up + lax.rem(1 - half + shift + up, 2)

    def owner_of(t):
        return lax.rem(CORES * chip + item_half(t) + strata - t, n)

    first_item = pltpu.make_async_copy(item_in, item_stage, load_i)
    first_user = pltpu.make_async_copy(user_in, users.at[0], load_u)

    def coded(b):
        return jnp.where(seen_stage[b % n] != 0, rate_stage[b % n], jnp.inf)

    def send_code(b):
        if b < n:
            for load in loads(b):
                load.wait()
        if b in (1, n - 1, n):
            stays = block_place(me, b) == me

            @pl.when(stays)
            def _():
                code[b] = coded(b)

            @pl.when(jnp.logical_not(stays))
            def _():
                code_send[b] = coded(b)
                code_copy(b).start()
        else:
            code_send[b] = coded(b)
            (relay_in if b in relayed else code_copy)(b).start()

    def traffic(t):
        for when in sorted(set(SEND_AT.values())):
            @pl.when(t == when)
            def _():
                for b in sorted(SEND_AT):
                    if SEND_AT[b] == when:
                        send_code(b)
        for b in relayed:
            @pl.when(t == RELAY_AT[b])
            def _():
                relay_in(b).wait_recv()
                relay_out(b).start()

    barrier = pltpu.get_barrier_semaphore()
    for offset in range(1, n):
        pl.semaphore_signal(barrier, inc=1, device_id=at(lax.rem(me + offset, n)), device_id_type=MESH)
    first_item.start()
    for load in loads(0):
        load.start()
    first_user.start()
    for b in sorted(range(1, n), key=lambda b: SEND_AT[b]):
        for load in loads(b):
            load.start()
    first_item.wait()
    first = item_stage[...].T
    items[0] = first
    items_bf[0] = first.astype(jnp.bfloat16)
    for load in loads(0):
        load.wait()
    code[0] = coded(0)
    pl.semaphore_wait(barrier, n - 1)

    def stratum(t):
        fixed = isinstance(t, int)
        start, end = fixed and t == 0, fixed and t == strata - 1
        half = item_half(t)
        target = user_next(t)
        user_stays = target == me
        item_stays = odd_chip if start or end else 0
        user_from_far = half == 0
        if fixed and t == 1:
            user_from_far = jnp.logical_or(user_from_far, odd_chip == 1)
        item_swapped = odd_chip == 0 if fixed and t == 1 else None

        if not (fixed and t > n):
            pl.when(t <= n)(functools.partial(traffic, t))

            @pl.when(jnp.logical_and(jnp.logical_and(t > 0, t <= n), owner_of(t) != me))
            def _():
                code_copy(t).wait_recv()

        if start:
            first_user.wait()
        else:
            @pl.when(user_from_far)
            def _():
                user_copy(t - 1, partner).wait_recv()

            if item_swapped is None:
                bf_copy(t - 1).wait_recv()
            else:
                @pl.when(item_swapped)
                def _():
                    bf_copy(t - 1).wait_recv()
                    item_copy(t - 1).wait_recv()

        slot = jnp.where(t > n, t - n, t)
        user = users[t]
        user_bf = user.astype(jnp.bfloat16)
        for step in range(STRATUM_STEPS):
            final = step == STRATUM_STEPS - 1
            pred = jnp.dot(user_bf, items_bf[t], preferred_element_type=jnp.float32)
            rate = code[slot]
            err = jnp.where(rate < jnp.inf, pred - rate, 0.0).astype(jnp.bfloat16)
            user = (1.0 - step_size * weight_decay) * user
            for h in range(2):
                cols = slice(h * n_items // 2, (h + 1) * n_items // 2)
                grad = lax.dot_general(
                    err[:, cols], items_bf[t, :, cols], (((1,), (1,)), ((), ())), preferred_element_type=jnp.float32)
                user = user - step_size * grad
            user_bf = user.astype(jnp.bfloat16)
            if final:
                users[t + user_stays.astype(jnp.int32)] = user

                @pl.when(jnp.logical_not(user_stays))
                def _():
                    user_copy(t, target).start()
            pred = jnp.dot(user_bf, items_bf[t], preferred_element_type=jnp.float32)
            rate = code[slot]
            err = jnp.where(rate < jnp.inf, pred - rate, 0.0).astype(jnp.bfloat16)
            grad = lax.dot_general(user_bf, err, (((0,), (0,)), ((), ())), preferred_element_type=jnp.float32)
            if step == 0 and not start and item_swapped is None:
                item_copy(t - 1).wait_recv()
            item = (1.0 - step_size * weight_decay) * items[t] - step_size * grad
            out = t + item_stays if final else t
            if not (final and end):
                items_bf[out] = item.astype(jnp.bfloat16)
            items[out] = item

        if start or end:
            @pl.when(item_stays == 0)
            def _():
                if start:
                    bf_copy(t).start()
                item_copy(t).start()
        else:
            bf_copy(t).start()
            item_copy(t).start()

    stratum(0)
    stratum(1)
    pl.loop(2, strata - 1)(stratum)
    stratum(strata - 1)

    @pl.when(odd_chip == 0)
    def _():
        item_copy(strata - 1).wait_recv()

    item_out[...] = items[strata]

    @pl.when(jnp.logical_or(core == 0, odd_chip == 1))
    def _():
        user_copy(strata - 1, partner).wait_recv()

    user_out[...] = users[strata]

    def drain(t):
        @pl.when(user_next(t) != me)
        def _():
            user_copy(t, partner).wait_send()

        if isinstance(t, int):
            @pl.when(odd_chip == 0)
            def _():
                if t == 0:
                    bf_copy(t).wait_send()
                item_copy(t).wait_send()
        else:
            bf_copy(t).wait_send()
            item_copy(t).wait_send()

    drain(0)
    pl.loop(1, strata - 1)(drain)
    drain(strata - 1)

    @pl.loop(1, n + 1)
    def _(b):
        @pl.when(block_place(me, b) != me)
        def _():
            code_copy(b).wait_send()

    for b in relayed:
        relay_in(b).wait_send()


def solution(mesh):
    n = mesh.shape["shard"]
    row_spec = P(("rep", "shard"), None)

    def local(ratings, observed, user_init, item_init):
        users_dev = ratings.shape[0]
        items_dev, rank = item_init.shape
        step_size = 0.5 / ((users_dev + items_dev + rank) / math.sqrt(rank))
        weight_decay = 0.03 * math.sqrt(users_dev * items_dev / rank)
        strata = EPOCHS * n
        relays = max(1, len(RELAY_AT))
        vmem = pl.BlockSpec(memory_space=pltpu.VMEM)
        anywhere = pl.BlockSpec(memory_space=pl.ANY)
        dma = pltpu.SemaphoreType.DMA
        user_out, item_out = pl.pallas_call(
            functools.partial(kernel, n, step_size, weight_decay),
            out_shape=(
                jax.ShapeDtypeStruct((users_dev, rank), jnp.float32),
                jax.ShapeDtypeStruct((rank, items_dev), jnp.float32),
            ),
            in_specs=[anywhere] * 4,
            out_specs=(vmem, vmem),
            scratch_shapes=[
                pltpu.VMEM((n, users_dev, items_dev), jnp.float32),
                pltpu.VMEM((n, users_dev, items_dev), jnp.int32),
                pltpu.VMEM((n + 1, users_dev, items_dev), jnp.float32),
                pltpu.VMEM((n + 1, users_dev, items_dev), jnp.float32),
                pltpu.VMEM((relays, users_dev, items_dev), jnp.float32),
                pltpu.VMEM((items_dev, rank), jnp.float32),
                pltpu.VMEM((strata + 1, rank, items_dev), jnp.float32),
                pltpu.VMEM((strata, rank, items_dev), jnp.bfloat16),
                pltpu.VMEM((strata + 1, users_dev, rank), jnp.float32),
                dma((n,)), dma((n,)), dma, dma, dma((n + 1,)), dma((n + 1,)), dma((relays,)), dma((relays,)),
                dma((strata,)), dma((strata,)), dma((strata,)), dma((strata,)), dma((strata,)), dma((strata,)),
            ],
            compiler_params=pltpu.CompilerParams(collective_id=0, has_side_effects=True),
        )(ratings, observed, user_init, item_init)
        return user_out, item_out.T

    return jax.shard_map(local, mesh=mesh, in_specs=(row_spec,) * 4, out_specs=(row_spec, row_spec), check_vma=False)
```

time: 160 us -> 148 us (0.925)
  Pallas kernels: 156 us -> 144 us
    pallas_call x1, Pallas kernels: 156 us -> 144 us  [local(): pl.pallas_call(functools.partial(kernel, n, step_size, weight_decay), out...]
where the time goes in v3:
time: 148 us
  Pallas kernels  144 us (97%)
  local copies, waits for them, and re-layouts  3.16 us (2%)
    pallas_call x1, Pallas kernels, local(): pl.pallas_call(functools.partial(kernel, n, step_size, weight_decay), out...  144 us
    unnamed x2, local copies, waits for them, and re-layouts  3.16 us

profile of v3, /device:TPU:21, one launch (start us, length us, event | category | flops | bytes accessed | tf_op | source)
XLA Modules:
  0.0 147.8 jit_solution(13297718222073706453)
XLA Ops:
  0.6 144.0 %shard_map.59 = (f32[64,128]{1,0:T(8,128)}, f32[128,512]{1,0:T(8,128)}) custom-call(f32[64,8192]{1,0:T(8,128)} %ratings.1, s32[64,8192]{1,0:T(8,128)} %observed.1, f32[64,128]{1,0:T(8,128)} %user_in.1, f32[512,128]{1,0:T(8,128)} %item_in.1), custom_call_target="tpu_custom_call" | custom-call | tf_op jit(solution)/shard_map/pallas_call | solution.py:292
  144.6 1.8 %copy.6 = f32[512,128]{1,0:T(8,128)} copy(f32[512,128]{0,1:T(8,128)} %bitcast.1) | data formatting | bytes 524288
  146.4 1.4 copy.8

commit v4 on v3

--- a/solution.py
+++ b/solution.py
@@ -11,9 +11,9 @@
 STRATUM_STEPS = 4
 EPOCHS = 2
 CORES = 2
-RELAY_HOP = 4
-SEND_AT = {1: 0, 2: 0, 3: 1, 4: 3, 5: 2, 6: 4, 7: 0, 8: 0, 9: 4, 10: 1, 11: 7, 12: 8, 13: 9, 14: 13, 15: 12, 16: 14}
-RELAY_AT = {7: 1, 8: 2}
+PIECES = 1
+SEND_AT = {(1, 0): 0, (2, 0): 1, (3, 0): 0, (4, 0): 2, (5, 0): 3, (6, 0): 5, (7, 0): 1, (8, 0): 3, (9, 0): 6, (10, 0): 0, (11, 0): 7, (12, 0): 7, (13, 0): 10, (14, 0): 13, (15, 0): 11, (16, 0): 14}
+RELAY = {(7, 0): (4, 4), (8, 0): (4, 5)}
 MESH = pl.DeviceIdType.MESH
 
 
@@ -24,6 +24,7 @@
     item_ss, item_rs, bf_ss, bf_rs,
 ):
     n_items = item_in.shape[0]
+    rows = user_in.shape[0] // PIECES
     strata = EPOCHS * n
     chips = n // CORES
     me = lax.axis_index("shard")
@@ -31,10 +32,13 @@
     core = lax.rem(me, CORES)
     odd_chip = lax.rem(chip, 2)
     partner = me + 1 - 2 * core
-    relayed = sorted(RELAY_AT)
+    relayed = sorted(RELAY)
 
     def at(device):
         return {"shard": device}
+
+    def shifted(offset):
+        return at(lax.rem(me + n + offset, n))
 
     def block_place(owner, b):
         item = lax.rem(owner + b, n)
@@ -48,21 +52,25 @@
             pltpu.make_async_copy(observed.at[:, pl.ds(col, n_items)], seen_stage.at[slot], load_m.at[slot]),
         )
 
-    def code_copy(b):
-        return pltpu.make_async_remote_copy(
-            src_ref=code_send.at[b], dst_ref=code.at[b], send_sem=code_ss.at[b], recv_sem=code_rs.at[b],
-            device_id=at(block_place(me, b)), device_id_type=MESH)
-
-    def relay_in(b):
-        r = relayed.index(b)
-        return pltpu.make_async_remote_copy(
-            src_ref=code_send.at[b], dst_ref=relay.at[r], send_sem=relay_ss.at[r], recv_sem=relay_rs.at[r],
-            device_id=at(lax.rem(me + n - RELAY_HOP, n)), device_id_type=MESH)
-
-    def relay_out(b):
-        return pltpu.make_async_remote_copy(
-            src_ref=relay.at[relayed.index(b)], dst_ref=code.at[b], send_sem=code_ss.at[b], recv_sem=code_rs.at[b],
-            device_id=at(block_place(lax.rem(me + RELAY_HOP, n), b)), device_id_type=MESH)
+    def part(h):
+        return pl.ds(h * rows, rows)
+
+    def code_copy(b, h, device):
+        return pltpu.make_async_remote_copy(
+            src_ref=code_send.at[b, part(h)], dst_ref=code.at[b, part(h)], send_sem=code_ss.at[b, h],
+            recv_sem=code_rs.at[b, h], device_id=at(device), device_id_type=MESH)
+
+    def relay_in(b, h):
+        r = relayed.index((b, h))
+        return pltpu.make_async_remote_copy(
+            src_ref=code_send.at[b, part(h)], dst_ref=relay.at[r], send_sem=relay_ss.at[r], recv_sem=relay_rs.at[r],
+            device_id=shifted(-RELAY[b, h][0]), device_id_type=MESH)
+
+    def relay_out(b, h):
+        owner = lax.rem(me + RELAY[b, h][0], n)
+        return pltpu.make_async_remote_copy(
+            src_ref=relay.at[relayed.index((b, h))], dst_ref=code.at[b, part(h)], send_sem=code_ss.at[b, h],
+            recv_sem=code_rs.at[b, h], device_id=at(block_place(owner, b)), device_id_type=MESH)
 
     def user_copy(t, device):
         return pltpu.make_async_remote_copy(
@@ -87,10 +95,9 @@
     def user_next(t):
         half = item_half(t)
         up = lax.rem(chip + half, chips)
-        shift = t + 1
         if isinstance(t, int) and t + 1 == strata:
-            return CORES * up + lax.rem(1 - half + shift, 2)
-        return CORES * up + lax.rem(1 - half + shift + up, 2)
+            return CORES * up + lax.rem(1 - half + t + 1, 2)
+        return CORES * up + lax.rem(1 - half + t + 1 + up, 2)
 
     def owner_of(t):
         return lax.rem(CORES * chip + item_half(t) + strata - t, n)
@@ -98,11 +105,11 @@
     first_item = pltpu.make_async_copy(item_in, item_stage, load_i)
     first_user = pltpu.make_async_copy(user_in, users.at[0], load_u)
 
-    def coded(b):
-        return jnp.where(seen_stage[b % n] != 0, rate_stage[b % n], jnp.inf)
-
-    def send_code(b):
-        if b < n:
+    def coded(b, h):
+        return jnp.where(seen_stage[b % n, part(h)] != 0, rate_stage[b % n, part(h)], jnp.inf)
+
+    def send_code(b, h):
+        if b < n and all(SEND_AT[b, h] < SEND_AT[b, g] or (SEND_AT[b, h] == SEND_AT[b, g] and h <= g) for g in range(PIECES)):
             for load in loads(b):
                 load.wait()
         if b in (1, n - 1, n):
@@ -110,37 +117,44 @@
 
             @pl.when(stays)
             def _():
-                code[b] = coded(b)
+                code[b, part(h)] = coded(b, h)
 
             @pl.when(jnp.logical_not(stays))
             def _():
-                code_send[b] = coded(b)
-                code_copy(b).start()
+                code_send[b, part(h)] = coded(b, h)
+                code_copy(b, h, block_place(me, b)).start()
         else:
-            code_send[b] = coded(b)
-            (relay_in if b in relayed else code_copy)(b).start()
+            code_send[b, part(h)] = coded(b, h)
+            if (b, h) in relayed:
+                relay_in(b, h).start()
+            else:
+                code_copy(b, h, block_place(me, b)).start()
+
+    def send_all(when):
+        for b, h in sorted(SEND_AT):
+            if SEND_AT[b, h] == when:
+                send_code(b, h)
 
     def traffic(t):
-        for when in sorted(set(SEND_AT.values())):
-            @pl.when(t == when)
-            def _():
-                for b in sorted(SEND_AT):
-                    if SEND_AT[b] == when:
-                        send_code(b)
-        for b in relayed:
-            @pl.when(t == RELAY_AT[b])
-            def _():
-                relay_in(b).wait_recv()
-                relay_out(b).start()
+        for when in sorted(set(SEND_AT.values()) - {0}):
+            pl.when(t == when)(functools.partial(send_all, when))
+        for b, h in relayed:
+            @pl.when(t == RELAY[b, h][1])
+            def _():
+                relay_in(b, h).wait_recv()
+                relay_out(b, h).start()
 
     barrier = pltpu.get_barrier_semaphore()
     for offset in range(1, n):
-        pl.semaphore_signal(barrier, inc=1, device_id=at(lax.rem(me + offset, n)), device_id_type=MESH)
+        pl.semaphore_signal(barrier, inc=1, device_id=shifted(offset), device_id_type=MESH)
+    order = sorted(range(1, n), key=lambda b: min(SEND_AT[b, h] for h in range(PIECES)))
+    early = [b for b in order if min(SEND_AT[b, h] for h in range(PIECES)) == 0]
+    for b in early + [0]:
+        for load in loads(b):
+            load.start()
     first_item.start()
-    for load in loads(0):
-        load.start()
     first_user.start()
-    for b in sorted(range(1, n), key=lambda b: SEND_AT[b]):
+    for b in order[len(early):]:
         for load in loads(b):
             load.start()
     first_item.wait()
@@ -149,8 +163,10 @@
     items_bf[0] = first.astype(jnp.bfloat16)
     for load in loads(0):
         load.wait()
-    code[0] = coded(0)
+    for h in range(PIECES):
+        code[0, part(h)] = coded(0, h)
     pl.semaphore_wait(barrier, n - 1)
+    send_all(0)
 
     def stratum(t):
         fixed = isinstance(t, int)
@@ -164,12 +180,13 @@
             user_from_far = jnp.logical_or(user_from_far, odd_chip == 1)
         item_swapped = odd_chip == 0 if fixed and t == 1 else None
 
-        if not (fixed and t > n):
+        if not start and not (fixed and t > n):
             pl.when(t <= n)(functools.partial(traffic, t))
 
-            @pl.when(jnp.logical_and(jnp.logical_and(t > 0, t <= n), owner_of(t) != me))
-            def _():
-                code_copy(t).wait_recv()
+            @pl.when(jnp.logical_and(t <= n, owner_of(t) != me))
+            def _():
+                for h in range(PIECES):
+                    code_copy(t, h, partner).wait_recv()
 
         if start:
             first_user.wait()
@@ -234,45 +251,61 @@
     pl.loop(2, strata - 1)(stratum)
     stratum(strata - 1)
 
-    @pl.when(odd_chip == 0)
-    def _():
-        item_copy(strata - 1).wait_recv()
-
-    item_out[...] = items[strata]
-
-    @pl.when(jnp.logical_or(core == 0, odd_chip == 1))
-    def _():
-        user_copy(strata - 1, partner).wait_recv()
-
-    user_out[...] = users[strata]
-
     def drain(t):
         @pl.when(user_next(t) != me)
         def _():
             user_copy(t, partner).wait_send()
 
-        if isinstance(t, int):
-            @pl.when(odd_chip == 0)
-            def _():
-                if t == 0:
-                    bf_copy(t).wait_send()
-                item_copy(t).wait_send()
-        else:
-            bf_copy(t).wait_send()
-            item_copy(t).wait_send()
-
-    drain(0)
+        bf_copy(t).wait_send()
+        item_copy(t).wait_send()
+
     pl.loop(1, strata - 1)(drain)
-    drain(strata - 1)
 
     @pl.loop(1, n + 1)
     def _(b):
         @pl.when(block_place(me, b) != me)
         def _():
-            code_copy(b).wait_send()
-
-    for b in relayed:
-        relay_in(b).wait_send()
+            for h in range(PIECES):
+                code_copy(b, h, partner).wait_send()
+
+    for b, h in relayed:
+        relay_in(b, h).wait_send()
+
+    @pl.when(user_next(0) != me)
+    def _():
+        user_copy(0, partner).wait_send()
+
+    @pl.when(odd_chip == 0)
+    def _():
+        bf_copy(0).wait_send()
+        item_copy(0).wait_send()
+        item_copy(strata - 1).wait_recv()
+
+    last_item = pltpu.make_async_copy(items.at[strata], item_out, load_i)
+    last_item.start()
+
+    @pl.when(jnp.logical_or(core == 0, odd_chip == 1))
+    def _():
+        user_copy(strata - 1, partner).wait_recv()
+
+    last_user = pltpu.make_async_copy(users.at[strata], user_out, load_u)
+    last_user.start()
+
+    @pl.when(user_next(strata - 1) != me)
+    def _():
+        user_copy(strata - 1, partner).wait_send()
+
+    @pl.when(odd_chip == 0)
+    def _():
+        item_copy(strata - 1).wait_send()
+
+    last_item.wait()
+    last_user.wait()
+
+
+def finish(user_in, item_in, user_out, item_out):
+    user_out[...] = user_in[...]
+    item_out[...] = item_in[...].T
 
 
 def solution(mesh):
@@ -285,7 +318,7 @@
         step_size = 0.5 / ((users_dev + items_dev + rank) / math.sqrt(rank))
         weight_decay = 0.03 * math.sqrt(users_dev * items_dev / rank)
         strata = EPOCHS * n
-        relays = max(1, len(RELAY_AT))
+        relays = max(1, len(RELAY))
         vmem = pl.BlockSpec(memory_space=pltpu.VMEM)
         anywhere = pl.BlockSpec(memory_space=pl.ANY)
         dma = pltpu.SemaphoreType.DMA
@@ -296,22 +329,30 @@
                 jax.ShapeDtypeStruct((rank, items_dev), jnp.float32),
             ),
             in_specs=[anywhere] * 4,
-            out_specs=(vmem, vmem),
+            out_specs=(anywhere, anywhere),
             scratch_shapes=[
                 pltpu.VMEM((n, users_dev, items_dev), jnp.float32),
                 pltpu.VMEM((n, users_dev, items_dev), jnp.int32),
                 pltpu.VMEM((n + 1, users_dev, items_dev), jnp.float32),
                 pltpu.VMEM((n + 1, users_dev, items_dev), jnp.float32),
-                pltpu.VMEM((relays, users_dev, items_dev), jnp.float32),
+                pltpu.VMEM((relays, users_dev // PIECES, items_dev), jnp.float32),
                 pltpu.VMEM((items_dev, rank), jnp.float32),
                 pltpu.VMEM((strata + 1, rank, items_dev), jnp.float32),
                 pltpu.VMEM((strata, rank, items_dev), jnp.bfloat16),
                 pltpu.VMEM((strata + 1, users_dev, rank), jnp.float32),
-                dma((n,)), dma((n,)), dma, dma, dma((n + 1,)), dma((n + 1,)), dma((relays,)), dma((relays,)),
+                dma((n,)), dma((n,)), dma, dma, dma((n + 1, PIECES)), dma((n + 1, PIECES)), dma((relays,)), dma((relays,)),
                 dma((strata,)), dma((strata,)), dma((strata,)), dma((strata,)), dma((strata,)), dma((strata,)),
             ],
             compiler_params=pltpu.CompilerParams(collective_id=0, has_side_effects=True),
         )(ratings, observed, user_init, item_init)
-        return user_out, item_out.T
+        return pl.pallas_call(
+            finish,
+            out_shape=(
+                jax.ShapeDtypeStruct((users_dev, rank), jnp.float32),
+                jax.ShapeDtypeStruct((items_dev, rank), jnp.float32),
+            ),
+            in_specs=[vmem, vmem],
+            out_specs=(vmem, vmem),
+        )(user_out, item_out)
 
     return jax.shard_map(local, mesh=mesh, in_specs=(row_spec,) * 4, out_specs=(row_spec, row_spec), check_vma=False)

time: 148 us -> 142 us (0.959)
  local copies, waits for them, and re-layouts: 3.16 us -> 0 us
  Pallas kernels: 144 us -> 141 us
    pallas_call x1, Pallas kernels: 144 us -> 139 us  [local(): pl.pallas_call(functools.partial(kernel, n, step_size, weight_decay), out...]
    unnamed x2 -> x0, local copies, waits for them, and re-layouts: 3.16 us -> none
    pallas_call x0 -> x1, Pallas kernels: none -> 1.81 us  [local(): pl.pallas_call(finish, out_shape=(jax.ShapeDtypeStruct((users_dev, rank),...]
where the time goes in v4:
time: 142 us
  Pallas kernels  141 us (99%)
    pallas_call x1, Pallas kernels, local(): pl.pallas_call(functools.partial(kernel, n, step_size, weight_decay), out...  139 us

profile of v4, /device:TPU:21, one launch (start us, length us, event | category | flops | bytes accessed | tf_op | source)
XLA Modules:
  0.0 141.9 jit_solution(15605040371084478074)
XLA Ops:
  0.6 139.5 %shard_map.59 = (f32[64,128]{1,0:T(8,128)}, f32[128,512]{1,0:T(8,128)}) custom-call(f32[64,8192]{1,0:T(8,128)} %ratings.1, s32[64,8192]{1,0:T(8,128)} %observed.1, f32[64,128]{1,0:T(8,128)} %user_in.1, f32[512,128]{1,0:T(8,128)} %item_in.1), custom_call_target="tpu_custom_call" | custom-call | tf_op jit(solution)/shard_map/pallas_call | solution.py:325
  140.1 1.8 %shard_map.60 = (f32[64,128]{1,0:T(8,128)}, f32[512,128]{1,0:T(8,128)}) custom-call(f32[64,128]{1,0:T(8,128)} %get-tuple-element.4.user_in, f32[128,512]{1,0:T(8,128)} %get-tuple-element.5.item_in), custom_call_target="tpu_custom_call" | custom-call | tf_op jit(solution)/shard_map/pallas_call | solution.py:348

commit v5 on v4

--- a/solution.py
+++ b/solution.py
@@ -12,7 +12,7 @@
 EPOCHS = 2
 CORES = 2
 PIECES = 1
-SEND_AT = {(1, 0): 0, (2, 0): 1, (3, 0): 0, (4, 0): 2, (5, 0): 3, (6, 0): 5, (7, 0): 1, (8, 0): 3, (9, 0): 6, (10, 0): 0, (11, 0): 7, (12, 0): 7, (13, 0): 10, (14, 0): 13, (15, 0): 11, (16, 0): 14}
+SEND_AT = {(1, 0): 0, (2, 0): 1, (3, 0): 0, (4, 0): 2, (5, 0): 3, (6, 0): 5, (7, 0): 1, (8, 0): 3, (9, 0): 6, (10, 0): 0, (11, 0): 7, (12, 0): 7, (13, 0): 10, (14, 0): 12, (15, 0): 11, (16, 0): 12}
 RELAY = {(7, 0): (4, 4), (8, 0): (4, 5)}
 MESH = pl.DeviceIdType.MESH
 

time: 142 us -> 142 us (level)
  no operation moved by 1% of the time
where the time goes in v5:
time: 142 us
  Pallas kernels  141 us (99%)
    pallas_call x1, Pallas kernels, local(): pl.pallas_call(functools.partial(kernel, n, step_size, weight_decay), out...  139 us

profile of v5, /device:TPU:21, one launch (start us, length us, event | category | flops | bytes accessed | tf_op | source)
XLA Modules:
  0.0 141.8 jit_solution(16424887591176648184)
XLA Ops:
  0.6 139.3 %shard_map.59 = (f32[64,128]{1,0:T(8,128)}, f32[128,512]{1,0:T(8,128)}) custom-call(f32[64,8192]{1,0:T(8,128)} %ratings.1, s32[64,8192]{1,0:T(8,128)} %observed.1, f32[64,128]{1,0:T(8,128)} %user_in.1, f32[512,128]{1,0:T(8,128)} %item_in.1), custom_call_target="tpu_custom_call" | custom-call | tf_op jit(solution)/shard_map/pallas_call | solution.py:325
  140.0 1.8 %shard_map.60 = (f32[64,128]{1,0:T(8,128)}, f32[512,128]{1,0:T(8,128)}) custom-call(f32[64,128]{1,0:T(8,128)} %get-tuple-element.4.user_in, f32[128,512]{1,0:T(8,128)} %get-tuple-element.5.item_in), custom_call_target="tpu_custom_call" | custom-call | tf_op jit(solution)/shard_map/pallas_call | solution.py:348

commit v6 on v5

--- a/solution.py
+++ b/solution.py
@@ -11,6 +11,7 @@
 STRATUM_STEPS = 4
 EPOCHS = 2
 CORES = 2
+TILES = 2
 PIECES = 1
 SEND_AT = {(1, 0): 0, (2, 0): 1, (3, 0): 0, (4, 0): 2, (5, 0): 3, (6, 0): 5, (7, 0): 1, (8, 0): 3, (9, 0): 6, (10, 0): 0, (11, 0): 7, (12, 0): 7, (13, 0): 10, (14, 0): 12, (15, 0): 11, (16, 0): 12}
 RELAY = {(7, 0): (4, 4), (8, 0): (4, 5)}
@@ -351,8 +352,15 @@
                 jax.ShapeDtypeStruct((users_dev, rank), jnp.float32),
                 jax.ShapeDtypeStruct((items_dev, rank), jnp.float32),
             ),
-            in_specs=[vmem, vmem],
-            out_specs=(vmem, vmem),
+            grid=(TILES,),
+            in_specs=[
+                pl.BlockSpec((users_dev // TILES, rank), lambda i: (i, 0)),
+                pl.BlockSpec((rank, items_dev // TILES), lambda i: (0, i)),
+            ],
+            out_specs=(
+                pl.BlockSpec((users_dev // TILES, rank), lambda i: (i, 0)),
+                pl.BlockSpec((items_dev // TILES, rank), lambda i: (i, 0)),
+            ),
         )(user_out, item_out)
 
     return jax.shard_map(local, mesh=mesh, in_specs=(row_spec,) * 4, out_specs=(row_spec, row_spec), check_vma=False)

time: 142 us -> 142 us (level)
  no operation moved by 1% of the time
where the time goes in v6:
time: 142 us
  Pallas kernels  141 us (99%)
    pallas_call x1, Pallas kernels, local(): pl.pallas_call(functools.partial(kernel, n, step_size, weight_decay), out...  139 us

profile of v6, /device:TPU:21, one launch (start us, length us, event | category | flops | bytes accessed | tf_op | source)
XLA Modules:
  0.0 141.8 jit_solution(10940507461584876239)
XLA Ops:
  0.6 139.3 %shard_map.59 = (f32[64,128]{1,0:T(8,128)}, f32[128,512]{1,0:T(8,128)}) custom-call(f32[64,8192]{1,0:T(8,128)} %ratings.1, s32[64,8192]{1,0:T(8,128)} %observed.1, f32[64,128]{1,0:T(8,128)} %user_in.1, f32[512,128]{1,0:T(8,128)} %item_in.1), custom_call_target="tpu_custom_call" | custom-call | tf_op jit(solution)/shard_map/pallas_call | solution.py:326
  140.0 1.8 %shard_map.60 = (f32[64,128]{1,0:T(8,128)}, f32[512,128]{1,0:T(8,128)}) custom-call(f32[64,128]{1,0:T(8,128)} %get-tuple-element.4.user_in, f32[128,512]{1,0:T(8,128)} %get-tuple-element.5.item_in), custom_call_target="tpu_custom_call" | custom-call | tf_op jit(solution)/shard_map/pallas_call | solution.py:349
